TPU v7x, 32 devices: a whole 2x2x4 slice. The times are simulated.
32 devices in a mesh: dp: 8 (over y, x, core), tensor: 4 (over z).
Axes of the slice: x: 2, y: 2, z: 4, core: 2. Of those that a mesh axis runs over, the one named last changes fastest.
Arguments:
- saved_input: bfloat16 [2048, 6144], P('dp', 'tensor'), may hold values from -6 to 6
- queries: bfloat16 [2048, 1024], P('dp', 'tensor'), may hold values from -8 to 8
- keys: bfloat16 [2048, 1024], P('dp', 'tensor'), may hold values from -8 to 8
- value_weight: bfloat16 [6144, 1024], P(None, 'tensor'), may hold values from -0.109375 to 0.109375
- grad_attended: bfloat16 [2048, 1024], P('dp', 'tensor'), may hold values from -6 to 6
Outputs:
- grad_input: bfloat16 [2048, 6144], P('dp', 'tensor')
- grad_value_weight: float32 [6144, 1024], P('dp', 'tensor')
- grad_queries: bfloat16 [2048, 1024], P('dp', 'tensor')
- grad_keys: bfloat16 [2048, 1024], P('dp', 'tensor')
All inputs are finite; a program needn't handle non-finite values.
Results may differ from a plain program's by a relative error of at most 0.02.
Values may be sent and summed in bfloat16 or wider, within the bound.
A program may use at most 64 MiB of HBM per device.

v0:
```python
import jax
import jax.numpy as jnp
from jax import lax
from jax.sharding import PartitionSpec as P

HD = 128


def on_device(saved_input, queries, keys, value_weight, grad_attended):
    token_count = queries.shape[0]
    local_width = value_weight.shape[1]
    local_heads = local_width // HD
    score_scale = 1.0 / jnp.sqrt(jnp.float32(HD))
    full_input = lax.all_gather(saved_input, "tensor", axis=1, tiled=True)
    values = jnp.dot(full_input, value_weight, preferred_element_type=jnp.float32).astype(
        jnp.bfloat16
    )
    query_heads = queries.reshape(token_count, local_heads, HD)
    key_heads = keys.reshape(token_count, local_heads, HD)
    value_heads = values.reshape(token_count, local_heads, HD)
    grad_heads = grad_attended.reshape(token_count, local_heads, HD)
    scores = (
        jnp.einsum("qhd,khd->hqk", query_heads, key_heads, preferred_element_type=jnp.float32)
        * score_scale
    )
    positions = lax.iota(jnp.int32, token_count)
    causal = positions[:, None] >= positions[None, :]
    scores = jnp.where(causal[None], scores, -jnp.inf)
    row_max = jnp.max(scores, axis=-1, keepdims=True)
    weights_exp = jnp.exp(scores - row_max)
    attention = weights_exp / jnp.sum(weights_exp, axis=-1, keepdims=True)
    probs_half = attention.astype(jnp.bfloat16)
    grad_values = jnp.einsum(
        "hqk,qhd->khd", probs_half, grad_heads, preferred_element_type=jnp.float32
    ).astype(jnp.bfloat16)
    grad_probs = jnp.einsum(
        "qhd,khd->hqk", grad_heads, value_heads, preferred_element_type=jnp.float32
    )
    row_dot = jnp.sum(attention * grad_probs, axis=-1, keepdims=True)
    grad_scores = (attention * (grad_probs - row_dot) * score_scale).astype(jnp.bfloat16)
    grad_queries = jnp.einsum(
        "hqk,khd->qhd", grad_scores, key_heads, preferred_element_type=jnp.float32
    ).astype(jnp.bfloat16)
    grad_keys = jnp.einsum(
        "hqk,qhd->khd", grad_scores, query_heads, preferred_element_type=jnp.float32
    ).astype(jnp.bfloat16)
    value_flat = grad_values.reshape(token_count, local_width)
    data_groups = lax.axis_size("dp")
    partial_value = lax.dot_general(
        value_flat, value_weight, (((1,), (1,)), ((), ())), preferred_element_type=jnp.float32
    )
    grad_input = lax.psum_scatter(
        partial_value.astype(jnp.bfloat16), "tensor", scatter_dimension=1, tiled=True
    )
    partial_value = lax.dot_general(
        full_input, value_flat, (((0,), (0,)), ((), ())), preferred_element_type=jnp.float32
    )
    summed = lax.psum_scatter(
        partial_value.astype(jnp.bfloat16), "dp", scatter_dimension=0, tiled=True
    ).astype(jnp.float32)
    grad_value_weight = summed / jnp.float32(data_groups)
    return (
        grad_input,
        grad_value_weight,
        grad_queries.reshape(token_count, local_width),
        grad_keys.reshape(token_count, local_width),
    )


def solution(mesh):
    placed = (
        P("dp", "tensor"),
        P("dp", "tensor"),
        P("dp", "tensor"),
        P(None, "tensor"),
        P("dp", "tensor"),
    )
    return jax.shard_map(
        on_device,
        mesh=mesh,
        in_specs=placed,
        out_specs=(P("dp", "tensor"), P("dp", "tensor"), P("dp", "tensor"), P("dp", "tensor")),
        check_vma=False,
    )
```

profile of v0, /device:TPU:0, one launch (start us, length us, event | category | flops | bytes accessed | tf_op | source)
XLA Modules:
  0.0 195.0 jit_solution(18344579385633237910)
XLA Ops:
  7.2 0.0 copy-start
  7.2 0.0 all-gather.2.cloned.1.call-start
  7.2 0.7 all-gather.2.cloned.1.call-update
  7.9 0.0 reduce-scatter.5.cloned.1.call-start
  8.0 1.2 copy.26
  9.1 1.0 copy.27
  10.2 0.0 copy-start.2
  10.2 1.2 fusion.28
  11.3 0.0 copy-done.2
  11.3 1.5 convolution_convert_fusion.4
  12.9 62.9 %all-gather.2.cloned.1.call-done = bf16[256,6144]{1,0:T(8,128)(2,1)} async-done(((bf16[256,1536]{1,0:T(8,128)(2,1)}), bf16[256,6144]{1,0:T(8,128)(2,1)}) %all-gather.2.cloned.1.call-update) | async-done | bytes 3145744 | tf_op jit(solution)/shard_map/all_gather | solution.py:14
  75.8 4.6 %fusion.2 = bf16[6144,256]{0,1:T(8,128)(2,1)} fusion(bf16[256,256]{0,1:T(8,128)(2,1)S(1)} %bitcast.41, bf16[256,6144]{1,0:T(8,128)(2,1)} %all-gather.2.cloned.1.call-done), kind=kOutput, calls=%fused_computation.4 | convolution fusion | flops 806879232 | bytes 6422528 | tf_op jit(solution)/shard_map/dot_general | solution.py:55
  80.3 0.0 reduce-scatter.5.cloned.1.call-update
  80.4 0.0 reduce-scatter.3.cloned.1.call-start
  80.4 0.0 copy-done
  80.4 2.7 %convolution_convert_fusion.1 = bf16[256,6144]{1,0:T(8,128)(2,1)} fusion(bf16[256,256]{0,1:T(8,128)(2,1)S(1)} %bitcast.42, bf16[6144,256]{1,0:T(8,128)(2,1)S(1)} %copy-done), kind=kOutput, calls=%fused_computation.3 | convolution fusion | flops 806879232 | bytes 6422528 | tf_op jit(solution)/shard_map/dot_general | solution.py:49
  83.1 0.0 reduce-scatter.3.cloned.1.call-update
  83.2 0.0 copy-start.1
  83.2 3.5 %convolution_convert_fusion.5 = bf16[256,256]{0,1:T(8,128)(2,1)S(1)} fusion(bf16[256,6144]{1,0:T(8,128)(2,1)} %all-gather.2.cloned.1.call-done, bf16[6144,256]{1,0:T(8,128)(2,1)S(1)} %copy-done), kind=kOutput, calls=%fused_computation.17 | convolution fusion | flops 805371904 | bytes 6422528 | tf_op jit(solution)/shard_map/dot_general | solution.py:15
  86.7 0.0 copy-done.1
  86.7 1.1 convolution_bitcast_fusion
  87.8 2.0 %convolution_convert_fusion.2 = bf16[2,256,128]{1,2,0:T(8,128)(2,1)S(1)} fusion(bf16[256,2,128]{0,2,1:T(8,128)(2,1)S(1)} %bitcast.49, f32[2,256,256]{1,2,0:T(8,128)} %convolution_bitcast_fusion, f32[2,256,256]{1,2,0:T(8,128)} %get-tuple-element.9, f32[2,256]{1,0:T(2,128)S(1)} %get-tuple-element.8), kind=kOutput, calls=%fused_computation.14 | convolution fusion | flops 34538240 | bytes 1312768 | tf_op jit(solution)/shard_map/hqk,khd->qhd/dot_general | solution.py:41
  89.7 0.8 copy.20
  90.5 2.0 %convolution_convert_fusion.3 = bf16[2,256,128]{1,2,0:T(8,128)(2,1)S(1)} fusion(bf16[256,2,128]{0,2,1:T(8,128)(2,1)S(1)} %bitcast.46, f32[2,256,256]{1,2,0:T(8,128)} %convolution_bitcast_fusion, f32[2,256,256]{1,2,0:T(8,128)} %get-tuple-element.9, f32[2,256]{1,0:T(2,128)S(1)} %get-tuple-element.8), kind=kOutput, calls=%fused_computation.15 | convolution fusion | flops 34538240 | bytes 1312768 | tf_op jit(solution)/shard_map/hqk,qhd->khd/dot_general | solution.py:44
  92.5 0.8 copy.21
  93.2 32.0 %reduce-scatter.5.cloned.1.call-done = bf16[768,256]{0,1:T(8,128)(2,1)} async-done(((bf16[6144,256]{0,1:T(8,128)(2,1)}), bf16[768,256]{0,1:T(8,128)(2,1)}) %reduce-scatter.5.cloned.1.call-update) | async-done | bytes 393232 | tf_op jit(solution)/shard_map/reduce_scatter | solution.py:58
  125.2 1.9 convert_multiply_fusion
  127.1 2.3 %copy.19 = f32[768,256]{1,0:T(8,128)} copy(f32[768,256]{0,1:T(8,128)} %convert_multiply_fusion) | data formatting | bytes 1572864
  129.4 59.1 %reduce-scatter.3.cloned.1.call-done = bf16[256,1536]{1,0:T(8,128)(2,1)} async-done(((bf16[256,6144]{1,0:T(8,128)(2,1)}), bf16[256,1536]{1,0:T(8,128)(2,1)}) %reduce-scatter.3.cloned.1.call-update) | async-done | bytes 786448 | tf_op jit(solution)/shard_map/reduce_scatter | solution.py:52
  (1 shorter events, 0.0 us)
Async XLA Ops:
  7.2 73.2 %copy-start = (bf16[6144,256]{1,0:T(8,128)(2,1)S(1)}, bf16[6144,256]{1,0:T(8,128)(2,1)}, u32[]{:S(2)}) copy-start(bf16[6144,256]{1,0:T(8,128)(2,1)} %param.8) | copy-start | bytes 9437188
  7.2 68.6 %all-gather.2.cloned.1.call-start = ((), (), s32[]{:S(2)}) async-start(), calls=%async_computation.3 | async-start | bytes 3932160 | tf_op jit(solution)/shard_map/all_gather | solution.py:14
  7.9 117.3 %reduce-scatter.5.cloned.1.call-start = ((), (), s32[]{:S(2)}) async-start(), calls=%async_computation.4 | async-start | bytes 3538944 | tf_op jit(solution)/shard_map/reduce_scatter | solution.py:58
  10.2 1.2 copy-start.2
  80.4 108.1 %reduce-scatter.3.cloned.1.call-start = ((), (), s32[]{:S(2)}) async-start(), calls=%async_computation.2 | async-start | bytes 3932160 | tf_op jit(solution)/shard_map/reduce_scatter | solution.py:52
  83.2 3.5 %copy-start.1 = (bf16[256,256]{1,0:T(8,128)(2,1)S(1)}, bf16[256,256]{1,0:T(8,128)(2,1)}, u32[]{:S(2)}) copy-start(bf16[256,256]{1,0:T(8,128)(2,1)} %param.9) | copy-start | bytes 393220
Sparse Core Ops, SparseCore 0:
  9.6 66.1 all-gather.1
  80.5 44.6 reduce-scatter.4
  128.1 60.3 reduce-scatter.2
where the time goes:
time: 195 us
  waiting for transfers between devices  155 us (79%)
  matrix products  18.5 us (9%)
  between operations  13.8 us (7%)
  local copies, waits for them, and re-layouts  5.98 us (3%)
  other arithmetic  1.95 us (1%)
    all_gather x1, waiting for transfers between devices, on_device(): full_input = lax.all_gather(saved_input, 'tensor', axis=1, tiled=True)  62.9 us
    reduce_scatter x1, waiting for transfers between devices, on_device(): lax.psum_scatter(partial_value.astype(jnp.bfloat16), 'tensor', scatter_di...  59.1 us
    reduce_scatter x1, waiting for transfers between devices, on_device(): lax.psum_scatter(partial_value.astype(jnp.bfloat16), 'dp', scatter_dimens...  32 us
    dot_general x1, matrix products, on_device(): lax.dot_general(full_input, value_flat, (((0,), (0,)), ((), ())), preferr...  4.58 us
  transfers between devices with their start and end apart: 3, of which 3 were waited for; matrix products, arithmetic and copies ran while one was open for 11% of the time, Pallas kernels for 0%

commit v1 on v0

--- a/solution.py
+++ b/solution.py
@@ -1,9 +1,260 @@
+import functools
+
 import jax
 import jax.numpy as jnp
 from jax import lax
+from jax.experimental import pallas as pl
+from jax.experimental.pallas import tpu as pltpu
 from jax.sharding import PartitionSpec as P
 
 HD = 128
+
+
+def fused_kernel(
+    n, chips,
+    x, queries, keys, w, ga,
+    gi, gw, gq, gk,
+    wfull, gvall, xpart, xt, qsend, rsrecv, vsend, vrecv, zsend, zrecv, fin, probs,
+    send_sem, recv_sem,
+):
+    f32, bf16 = jnp.float32, jnp.bfloat16
+    tokens, feat = x.shape
+    width = w.shape[1]
+    half = feat // 2
+    wrows = feat // (2 * chips)
+    prows = half // chips
+    t = lax.axis_index("tensor")
+    d = lax.axis_index("dp")
+    c = d // 2
+    k = d % 2
+    scale = 1.0 / (HD ** 0.5)
+
+    def level(o):
+        return (d, lax.rem(t + o, n))
+
+    def below(o):
+        return (d, lax.rem(t + n - o, n))
+
+    def chip(q):
+        return (2 * lax.rem(c + q, chips) + k, t)
+
+    partner = (2 * c + 1 - k, t)
+    count = [0]
+    started = []
+
+    def copy(src, dst, device):
+        i = count[0]
+        count[0] += 1
+        return pltpu.make_async_remote_copy(
+            src_ref=src, dst_ref=dst, send_sem=send_sem.at[i], recv_sem=recv_sem.at[i],
+            device_id=device, device_id_type=pl.DeviceIdType.MESH,
+        )
+
+    def go(cp):
+        cp.start()
+        started.append(cp)
+
+    def rows(i, size):
+        return pl.ds(pl.multiple_of(i * size, size), size)
+
+    barrier = pltpu.get_barrier_semaphore()
+    peers = [level(o) for o in range(1, n)] + [chip(q) for q in range(1, chips)] + [partner]
+    for peer in peers:
+        pl.semaphore_signal(
+            barrier, inc=1, device_id=peer, device_id_type=pl.DeviceIdType.MESH
+        )
+    pl.semaphore_wait(barrier, len(peers))
+
+    wz = {}
+    for o in range(1, n):
+        first = lax.rem(t + o, n) * feat + d * wrows
+        wz[o] = copy(
+            w.at[pl.ds(pl.multiple_of(first, wrows), wrows)],
+            wfull.at[o - 1, rows(d, wrows)],
+            level(o),
+        )
+        go(wz[o])
+    xcp = copy(
+        x.at[:, pl.ds(pl.multiple_of((1 - k) * half, half), half)], xpart, partner
+    )
+    go(xcp)
+
+    row = lax.broadcasted_iota(jnp.int32, (tokens, tokens), 0)
+    col = lax.broadcasted_iota(jnp.int32, (tokens, tokens), 1)
+    causal = row >= col
+    heads = width // HD
+    for h in range(heads):
+        cols = slice(h * HD, (h + 1) * HD)
+        scores = lax.dot_general(
+            queries[:, cols], keys[:, cols], (((1,), (1,)), ((), ())),
+            preferred_element_type=f32,
+        ) * scale
+        scores = jnp.where(causal, scores, -jnp.inf)
+        e = jnp.exp(scores - jnp.max(scores, axis=-1, keepdims=True))
+        p = e / jnp.sum(e, axis=-1, keepdims=True)
+        probs[h] = p
+        gvall[0, 0:tokens, cols] = lax.dot_general(
+            p.astype(bf16), ga[:, cols], (((0,), (0,)), ((), ())),
+            preferred_element_type=f32,
+        ).astype(bf16)
+
+    gz, gd = {}, {}
+    for o in range(1, n):
+        gz[o] = copy(gvall.at[0, 0:tokens], gvall.at[o, 0:tokens], level(o))
+        go(gz[o])
+    gd[0] = copy(gvall.at[0, 0:tokens], gvall.at[0, tokens:2 * tokens], partner)
+    go(gd[0])
+
+    wp, wd = {}, {}
+    for o in range(1, n):
+        wz[o].wait_recv()
+        mine = wfull.at[o - 1, rows(d, wrows)]
+        for q in range(1, chips):
+            wp[o, q] = copy(mine, mine, chip(q))
+            go(wp[o, q])
+        wd[o, 0] = copy(mine, mine, partner)
+        go(wd[o, 0])
+
+    xt[:, 0:tokens] = x[:, pl.ds(pl.multiple_of(k * half, half), half)].T
+    xcp.wait_recv()
+    xt[:, tokens:2 * tokens] = xpart[...].T
+
+    rs = {}
+
+    def weight_term(o):
+        gd[o].wait_recv()
+        qsend[o] = jnp.dot(xt[...], gvall[o], preferred_element_type=f32).astype(bf16)
+        for q in range(1, chips):
+            rs[o, q] = copy(
+                qsend.at[o, rows(lax.rem(c + q, chips), prows)], rsrecv.at[q - 1, o], chip(q)
+            )
+            go(rs[o, q])
+
+    weight_term(0)
+    for o in range(1, n):
+        gz[o].wait_recv()
+        gd[o] = copy(
+            gvall.at[o, 0:tokens], gvall.at[o, tokens:2 * tokens], partner
+        )
+        go(gd[o])
+    for o in range(1, n):
+        weight_term(o)
+
+    for o in range(1, n):
+        for q in range(1, chips):
+            wp[o, q].wait_recv()
+            theirs = wfull.at[o - 1, rows(2 * lax.rem(c + chips - q, chips) + k, wrows)]
+            wd[o, q] = copy(theirs, theirs, partner)
+            go(wd[o, q])
+    vz = {}
+    for o in range(1, n):
+        for q in range(chips):
+            wd[o, q].wait_recv()
+        vsend[o - 1] = jnp.dot(
+            x[...], wfull[o - 1], preferred_element_type=f32
+        ).astype(bf16)
+        vz[o] = copy(vsend.at[o - 1], vrecv.at[o - 1], below(o))
+        go(vz[o])
+
+    az = {}
+    for o in list(range(1, n)) + [0]:
+        total = qsend[o, rows(c, prows)].astype(f32)
+        for q in range(1, chips):
+            rs[o, q].wait_recv()
+            total = total + rsrecv[q - 1, o].astype(f32)
+        if o == 0:
+            zrecv[0] = total.astype(bf16)
+        else:
+            zsend[o - 1] = total.astype(bf16)
+            az[o] = copy(zsend.at[o - 1], zrecv.at[o], below(o))
+            go(az[o])
+
+    own = rows(t, feat)
+    contract = (((1,), (1,)), ((), ()))
+    acc = lax.dot_general(
+        gvall[0, 0:tokens], w[own], contract, preferred_element_type=f32
+    )
+    for o in range(1, n):
+        acc = acc + lax.dot_general(
+            gvall[o, 0:tokens], wfull[o - 1], contract, preferred_element_type=f32
+        )
+    gi[...] = acc.astype(bf16)
+
+    values = jnp.dot(x[...], w[own], preferred_element_type=f32)
+    for o in range(1, n):
+        vz[o].wait_recv()
+        values = values + vrecv[o - 1].astype(f32)
+    values = values.astype(bf16)
+    for h in range(heads):
+        cols = slice(h * HD, (h + 1) * HD)
+        grad_probs = lax.dot_general(
+            ga[:, cols], values[:, cols], contract, preferred_element_type=f32
+        )
+        p = probs[h]
+        row_dot = jnp.sum(p * grad_probs, axis=-1, keepdims=True)
+        gs = (p * (grad_probs - row_dot) * scale).astype(bf16)
+        gq[:, cols] = jnp.dot(gs, keys[:, cols], preferred_element_type=f32).astype(bf16)
+        gk[:, cols] = lax.dot_general(
+            gs, queries[:, cols], (((0,), (0,)), ((), ())), preferred_element_type=f32
+        ).astype(bf16)
+
+    for o in range(1, n):
+        az[o].wait_recv()
+    fz = {}
+    for q in range(1, chips):
+        o = lax.rem(lax.rem(c + q, chips) + n - t, n)
+        fz[q] = copy(zrecv.at[o], fin.at[q], chip(q))
+        go(fz[q])
+    groups = float(2 * chips)
+    gw[rows(c, prows), :] = zrecv[lax.rem(c + n - t, n)].astype(f32) / groups
+    for q in range(1, chips):
+        fz[q].wait_recv()
+        gw[rows(lax.rem(c + chips - q, chips), prows), :] = fin[q].astype(f32) / groups
+    for cp in started:
+        cp.wait_send()
+
+
+def fused(n, groups, saved_input, queries, keys, value_weight, grad_attended):
+    chips = groups // 2
+    tokens, feat = saved_input.shape
+    depth, width = value_weight.shape
+    half, prows = feat // 2, feat // groups
+    bf16 = jnp.bfloat16
+    levels = n - 1
+    copies = (
+        levels * (3 + chips - 1 + chips) + 1 + n + n * (chips - 1) + levels + chips - 1
+    )
+    vmem = pl.BlockSpec(memory_space=pltpu.VMEM)
+    return pl.pallas_call(
+        functools.partial(fused_kernel, n, chips),
+        out_shape=(
+            jax.ShapeDtypeStruct((tokens, feat), bf16),
+            jax.ShapeDtypeStruct((depth // groups, width), jnp.float32),
+            jax.ShapeDtypeStruct(queries.shape, bf16),
+            jax.ShapeDtypeStruct(keys.shape, bf16),
+        ),
+        in_specs=[vmem] * 5,
+        out_specs=(vmem,) * 4,
+        scratch_shapes=[
+            pltpu.VMEM((levels, feat, width), bf16),
+            pltpu.VMEM((n, 2 * tokens, width), bf16),
+            pltpu.VMEM((tokens, half), bf16),
+            pltpu.VMEM((half, 2 * tokens), bf16),
+            pltpu.VMEM((n, half, width), bf16),
+            pltpu.VMEM((chips - 1, n, prows, width), bf16),
+            pltpu.VMEM((levels, tokens, width), bf16),
+            pltpu.VMEM((levels, tokens, width), bf16),
+            pltpu.VMEM((levels, prows, width), bf16),
+            pltpu.VMEM((n, prows, width), bf16),
+            pltpu.VMEM((chips, prows, width), bf16),
+            pltpu.VMEM((width // HD, tokens, tokens), jnp.float32),
+            pltpu.SemaphoreType.DMA((copies,)),
+            pltpu.SemaphoreType.DMA((copies,)),
+        ],
+        compiler_params=pltpu.CompilerParams(
+            collective_id=0, has_side_effects=True, vmem_limit_bytes=56 * 2**20
+        ),
+    )(saved_input, queries, keys, value_weight, grad_attended)
 
 
 def on_device(saved_input, queries, keys, value_weight, grad_attended):
@@ -75,8 +326,12 @@
         P(None, "tensor"),
         P("dp", "tensor"),
     )
+    levels, groups = mesh.shape["tensor"], mesh.shape["dp"]
+    run = on_device
+    if groups == 2 * levels and levels > 1:
+        run = functools.partial(fused, levels, groups)
     return jax.shard_map(
-        on_device,
+        run,
         mesh=mesh,
         in_specs=placed,
         out_specs=(P("dp", "tensor"), P("dp", "tensor"), P("dp", "tensor"), P("dp", "tensor")),

time: 195 us -> 65.8 us (0.34)
  waiting for transfers between devices: 155 us -> 0 us
  Pallas kernels: 0 us -> 59.5 us
  matrix products: 18.5 us -> 0 us
  between operations: 13.8 us -> 0.66 us
  other arithmetic: 1.95 us -> 0 us
    reduce_scatter x2 -> x0, waiting for transfers between devices: 91.1 us -> none  [the longest x1 59.1 us: on_device(): lax.psum_scatter(partial_value.astype(jnp.bfloat16), 'tensor', scatter_di...]
    all_gather x1 -> x0, waiting for transfers between devices: 62.9 us -> none  [on_device(): full_input = lax.all_gather(saved_input, 'tensor', axis=1, tiled=True)]
    pallas_call x0 -> x1, Pallas kernels: none -> 59.5 us  [fused(): pl.pallas_call(functools.partial(fused_kernel, n, chips), out_shape=(jax....]
    dot_general x7 -> x0, matrix products: 17.3 us -> none  [the longest x1 4.58 us: on_device(): lax.dot_general(full_input, value_flat, (((0,), (0,)), ((), ())), preferr...]
    reshape x2 -> x0, local copies, waits for them, and re-layouts: 2.16 us -> none  [the longest x1 1.16 us: on_device(): query_heads = queries.reshape(token_count, local_heads, HD)]
    unnamed x9 -> x8, local copies, waits for them, and re-layouts: 3.82 us -> 5.49 us
  transfers between devices with their start and end apart: 3 -> 0, of which waited for: 3 -> 0; matrix products, arithmetic and copies ran while one was open for 11% -> 0% of each run, Pallas kernels for 0% -> 0%
where the time goes in v1:
time: 65.8 us; the launch traced here: 65.6 us
  Pallas kernels  59.5 us (90%)
  local copies, waits for them, and re-layouts  5.49 us (8%)
  between operations  0.66 us (1%)
    pallas_call x1, Pallas kernels, fused(): pl.pallas_call(functools.partial(fused_kernel, n, chips), out_shape=(jax....  59.5 us
    unnamed x8, local copies, waits for them, and re-layouts  5.49 us

profile of v1, /device:TPU:0, one launch (start us, length us, event | category | flops | bytes accessed | tf_op | source)
XLA Modules:
  0.0 65.6 jit_solution(4562922268859422609)
XLA Ops:
  0.6 59.5 %shard_map.84 = (bf16[256,1536]{1,0:T(8,128)(2,1)}, f32[768,256]{1,0:T(8,128)}, bf16[256,256]{1,0:T(8,128)(2,1)}, bf16[256,256]{1,0:T(8,128)(2,1)}) custom-call(bf16[256,1536]{1,0:T(8,128)(2,1)} %x.1, bf16[256,256]{1,0:T(8,128)(2,1)} %queries.1, bf16[256,256]{1,0:T(8,128)(2,1)} %keys.1, bf16[6144,256]{1,0:T(8,128)(2,1)} %w.1, bf16[256,256]{1,0:T(8,128)(2,1)} %ga.1), custom_call_target="tpu_custom_call" | custom-call | tf_op jit(solution)/shard_map/pallas_call | solution.py:228
  60.1 0.0 copy-start.1
  60.1 0.0 copy-start
  60.1 2.1 %copy.13 = bf16[256,1536]{1,0:T(8,128)(2,1)} copy(bf16[256,1536]{1,0:T(8,128)(2,1)} %get-tuple-element.8) | data formatting | bytes 1572864
  62.2 2.1 %copy.14 = f32[768,256]{1,0:T(8,128)} copy(f32[768,256]{1,0:T(8,128)} %get-tuple-element.9) | data formatting | bytes 1572864
  64.3 0.0 copy-done.1
  64.3 0.7 copy.15
  65.0 0.0 copy-done
  65.0 0.7 copy.16
Async XLA Ops:
  60.1 4.2 %copy-start.1 = (bf16[256,256]{1,0:T(8,128)(2,1)S(1)}, bf16[256,256]{1,0:T(8,128)(2,1)}, u32[]{:S(2)}) copy-start(bf16[256,256]{1,0:T(8,128)(2,1)} %get-tuple-element.10) | copy-start | bytes 393220
  60.1 4.8 %copy-start = (bf16[256,256]{1,0:T(8,128)(2,1)S(1)}, bf16[256,256]{1,0:T(8,128)(2,1)}, u32[]{:S(2)}) copy-start(bf16[256,256]{1,0:T(8,128)(2,1)} %get-tuple-element.11) | copy-start | bytes 393220

commit v2 on v1

--- a/solution.py
+++ b/solution.py
@@ -14,8 +14,8 @@
     n, chips,
     x, queries, keys, w, ga,
     gi, gw, gq, gk,
-    wfull, gvall, xpart, xt, qsend, rsrecv, vsend, vrecv, zsend, zrecv, fin, probs,
-    send_sem, recv_sem,
+    wown, wfull, gvall, xpart, xt, qsend, rsrecv, vsend, vrecv, zsend, zrecv, fin, probs,
+    send_sem, recv_sem, own_sem, fin_send, fin_recv,
 ):
     f32, bf16 = jnp.float32, jnp.bfloat16
     tokens, feat = x.shape
@@ -66,7 +66,8 @@
     pl.semaphore_wait(barrier, len(peers))
 
     wz = {}
-    for o in range(1, n):
+
+    def send_weight(o):
         first = lax.rem(t + o, n) * feat + d * wrows
         wz[o] = copy(
             w.at[pl.ds(pl.multiple_of(first, wrows), wrows)],
@@ -74,10 +75,18 @@
             level(o),
         )
         go(wz[o])
+
+    early = [o for o in range(1, n) if o in (1, n - 1)]
+    late = [o for o in range(1, n) if o not in early]
+    for o in early:
+        send_weight(o)
+    own = rows(t, feat)
+    own_copy = pltpu.make_async_copy(w.at[own], wown, own_sem.at[0])
     xcp = copy(
         x.at[:, pl.ds(pl.multiple_of((1 - k) * half, half), half)], xpart, partner
     )
     go(xcp)
+    own_copy.start()
 
     row = lax.broadcasted_iota(jnp.int32, (tokens, tokens), 0)
     col = lax.broadcasted_iota(jnp.int32, (tokens, tokens), 1)
@@ -105,15 +114,8 @@
     gd[0] = copy(gvall.at[0, 0:tokens], gvall.at[0, tokens:2 * tokens], partner)
     go(gd[0])
 
-    wp, wd = {}, {}
-    for o in range(1, n):
-        wz[o].wait_recv()
-        mine = wfull.at[o - 1, rows(d, wrows)]
-        for q in range(1, chips):
-            wp[o, q] = copy(mine, mine, chip(q))
-            go(wp[o, q])
-        wd[o, 0] = copy(mine, mine, partner)
-        go(wd[o, 0])
+    for o in late:
+        send_weight(o)
 
     xt[:, 0:tokens] = x[:, pl.ds(pl.multiple_of(k * half, half), half)].T
     xcp.wait_recv()
@@ -131,6 +133,17 @@
             go(rs[o, q])
 
     weight_term(0)
+
+    wp, wd = {}, {}
+    for o in early + late:
+        wz[o].wait_recv()
+        mine = wfull.at[o - 1, rows(d, wrows)]
+        for q in range(1, chips):
+            wp[o, q] = copy(mine, mine, chip(q))
+            go(wp[o, q])
+        wd[o, 0] = copy(mine, mine, partner)
+        go(wd[o, 0])
+
     for o in range(1, n):
         gz[o].wait_recv()
         gd[o] = copy(
@@ -157,7 +170,7 @@
         go(vz[o])
 
     az = {}
-    for o in list(range(1, n)) + [0]:
+    for o in range(n):
         total = qsend[o, rows(c, prows)].astype(f32)
         for q in range(1, chips):
             rs[o, q].wait_recv()
@@ -169,10 +182,10 @@
             az[o] = copy(zsend.at[o - 1], zrecv.at[o], below(o))
             go(az[o])
 
-    own = rows(t, feat)
+    own_copy.wait()
     contract = (((1,), (1,)), ((), ()))
     acc = lax.dot_general(
-        gvall[0, 0:tokens], w[own], contract, preferred_element_type=f32
+        gvall[0, 0:tokens], wown[...], contract, preferred_element_type=f32
     )
     for o in range(1, n):
         acc = acc + lax.dot_general(
@@ -180,7 +193,7 @@
         )
     gi[...] = acc.astype(bf16)
 
-    values = jnp.dot(x[...], w[own], preferred_element_type=f32)
+    values = jnp.dot(x[...], wown[...], preferred_element_type=f32)
     for o in range(1, n):
         vz[o].wait_recv()
         values = values + vrecv[o - 1].astype(f32)
@@ -198,20 +211,46 @@
             gs, queries[:, cols], (((0,), (0,)), ((), ())), preferred_element_type=f32
         ).astype(bf16)
 
-    for o in range(1, n):
-        az[o].wait_recv()
-    fz = {}
+    def last(o, q):
+        return pltpu.make_async_remote_copy(
+            src_ref=zrecv.at[o], dst_ref=fin.at[c],
+            send_sem=fin_send.at[q], recv_sem=fin_recv.at[q],
+            device_id=(2 * lax.rem(c + q, chips) + k, t),
+            device_id_type=pl.DeviceIdType.MESH,
+        )
+
+    groups = float(2 * chips)
+    for o in range(n):
+        if o > 0:
+            az[o].wait_recv()
+        block = lax.rem(t + o, n)
+
+        @pl.when(block != c)
+        def _():
+            last(o, lax.rem(block + chips - c, chips)).start()
+
+        @pl.when(block == c)
+        def _():
+            gw[rows(c, prows), :] = zrecv[o].astype(f32) / groups
+
     for q in range(1, chips):
-        o = lax.rem(lax.rem(c + q, chips) + n - t, n)
-        fz[q] = copy(zrecv.at[o], fin.at[q], chip(q))
-        go(fz[q])
-    groups = float(2 * chips)
-    gw[rows(c, prows), :] = zrecv[lax.rem(c + n - t, n)].astype(f32) / groups
-    for q in range(1, chips):
-        fz[q].wait_recv()
-        gw[rows(lax.rem(c + chips - q, chips), prows), :] = fin[q].astype(f32) / groups
+        last(0, q).wait_recv()
+        theirs = lax.rem(c + chips - q, chips)
+        gw[rows(theirs, prows), :] = fin[theirs].astype(f32) / groups
+        last(0, q).wait_send()
     for cp in started:
         cp.wait_send()
+
+
+def write_out(*refs):
+    results, outs, sem = refs[:4], refs[4:8], refs[8]
+    moves = [
+        pltpu.make_async_copy(results[i], outs[i], sem.at[i]) for i in range(4)
+    ]
+    for move in moves:
+        move.start()
+    for move in moves:
+        move.wait()
 
 
 def fused(n, groups, saved_input, queries, keys, value_weight, grad_attended):
@@ -222,20 +261,21 @@
     bf16 = jnp.bfloat16
     levels = n - 1
     copies = (
-        levels * (3 + chips - 1 + chips) + 1 + n + n * (chips - 1) + levels + chips - 1
+        levels * (3 + chips - 1 + chips) + 1 + n + n * (chips - 1) + levels
     )
     vmem = pl.BlockSpec(memory_space=pltpu.VMEM)
-    return pl.pallas_call(
+    results = pl.pallas_call(
         functools.partial(fused_kernel, n, chips),
         out_shape=(
-            jax.ShapeDtypeStruct((tokens, feat), bf16),
-            jax.ShapeDtypeStruct((depth // groups, width), jnp.float32),
-            jax.ShapeDtypeStruct(queries.shape, bf16),
-            jax.ShapeDtypeStruct(keys.shape, bf16),
+            pltpu.VMEM((tokens, feat), bf16),
+            pltpu.VMEM((depth // groups, width), jnp.float32),
+            pltpu.VMEM(queries.shape, bf16),
+            pltpu.VMEM(keys.shape, bf16),
         ),
-        in_specs=[vmem] * 5,
+        in_specs=[vmem] * 3 + [pl.BlockSpec(memory_space=pl.ANY), vmem],
         out_specs=(vmem,) * 4,
         scratch_shapes=[
+            pltpu.VMEM((feat, width), bf16),
             pltpu.VMEM((levels, feat, width), bf16),
             pltpu.VMEM((n, 2 * tokens, width), bf16),
             pltpu.VMEM((tokens, half), bf16),
@@ -250,11 +290,22 @@
             pltpu.VMEM((width // HD, tokens, tokens), jnp.float32),
             pltpu.SemaphoreType.DMA((copies,)),
             pltpu.SemaphoreType.DMA((copies,)),
+            pltpu.SemaphoreType.DMA((1,)),
+            pltpu.SemaphoreType.DMA((chips,)),
+            pltpu.SemaphoreType.DMA((chips,)),
         ],
         compiler_params=pltpu.CompilerParams(
-            collective_id=0, has_side_effects=True, vmem_limit_bytes=56 * 2**20
+            collective_id=0, has_side_effects=True, vmem_limit_bytes=58 * 2**20
         ),
     )(saved_input, queries, keys, value_weight, grad_attended)
+    return pl.pallas_call(
+        write_out,
+        out_shape=tuple(jax.ShapeDtypeStruct(r.shape, r.dtype) for r in results),
+        in_specs=[vmem] * 4,
+        out_specs=(pl.BlockSpec(memory_space=pl.ANY),) * 4,
+        scratch_shapes=[pltpu.SemaphoreType.DMA((4,))],
+        compiler_params=pltpu.CompilerParams(vmem_limit_bytes=8 * 2**20),
+    )(*results)
 
 
 def on_device(saved_input, queries, keys, value_weight, grad_attended):

time: 65.8 us -> 59.6 us (0.906)
  the two profiles are of different devices: /device:TPU:0 before, /device:TPU:18 now
where the time goes in v2:
time: 59.6 us; the launch traced here: 59.4 us
  Pallas kernels  58.8 us (99%)
  between operations  0.64 us (1%)
    pallas_call x1, Pallas kernels, fused(): pl.pallas_call(functools.partial(fused_kernel, n, chips), out_shape=(pltp...  57.5 us
    pallas_call x1, Pallas kernels, fused(): pl.pallas_call(write_out, out_shape=tuple((jax.ShapeDtypeStruct(r.shape,...  1.25 us

profile of v2, /device:TPU:18, one launch (start us, length us, event | category | flops | bytes accessed | tf_op | source)
XLA Modules:
  0.0 59.4 jit_solution(17431553982278949674)
XLA Ops:
  0.6 57.5 %shard_map.84 = (bf16[256,1536]{1,0:T(8,128)(2,1)S(1)}, f32[768,256]{1,0:T(8,128)S(1)}, bf16[256,256]{1,0:T(8,128)(2,1)S(1)}, bf16[256,256]{1,0:T(8,128)(2,1)S(1)}) custom-call(bf16[256,1536]{1,0:T(8,128)(2,1)} %x.1, bf16[256,256]{1,0:T(8,128)(2,1)} %queries.1, bf16[256,256]{1,0:T(8,128)(2,1)} %keys.1, bf16[6144,256]{1,0:T(8,128)(2,1)} %w.1, bf16[256,256]{1,0:T(8,128)(2,1)} %ga.1), custom_call_target="tpu_custom_call" | custom-call | tf_op jit(solution)/shard_map/pallas_call | solution.py:267
  58.2 1.3 %shard_map.85 = (bf16[256,1536]{1,0:T(8,128)(2,1)}, f32[768,256]{1,0:T(8,128)}, bf16[256,256]{1,0:T(8,128)(2,1)}, bf16[256,256]{1,0:T(8,128)(2,1)}) custom-call(bf16[256,1536]{1,0:T(8,128)(2,1)S(1)} %get-tuple-element.8.refs_0_, f32[768,256]{1,0:T(8,128)S(1)} %get-tuple-element.9.refs_1_, bf16[256,256]{1,0:T(8,128)(2,1)S(1)} %get-tuple-element.10.refs_2_, ...), custom_call_target="tpu_custom_call" | custom-call | tf_op jit(solution)/shard_map/pallas_call | solution.py:301

commit v3 on v2

--- a/solution.py
+++ b/solution.py
@@ -76,7 +76,7 @@
         )
         go(wz[o])
 
-    early = [o for o in range(1, n) if o in (1, n - 1)]
+    early = list(range(1, n))
     late = [o for o in range(1, n) if o not in early]
     for o in early:
         send_weight(o)
@@ -193,6 +193,28 @@
         )
     gi[...] = acc.astype(bf16)
 
+    def last(o, q):
+        return pltpu.make_async_remote_copy(
+            src_ref=zrecv.at[o], dst_ref=fin.at[c],
+            send_sem=fin_send.at[q], recv_sem=fin_recv.at[q],
+            device_id=(2 * lax.rem(c + q, chips) + k, t),
+            device_id_type=pl.DeviceIdType.MESH,
+        )
+
+    groups = float(2 * chips)
+    for o in range(n):
+        if o > 0:
+            az[o].wait_recv()
+        block = lax.rem(t + o, n)
+
+        @pl.when(block != c)
+        def _():
+            last(o, lax.rem(block + chips - c, chips)).start()
+
+        @pl.when(block == c)
+        def _():
+            gw[rows(c, prows), :] = zrecv[o].astype(f32) / groups
+
     values = jnp.dot(x[...], wown[...], preferred_element_type=f32)
     for o in range(1, n):
         vz[o].wait_recv()
@@ -210,28 +232,6 @@
         gk[:, cols] = lax.dot_general(
             gs, queries[:, cols], (((0,), (0,)), ((), ())), preferred_element_type=f32
         ).astype(bf16)
-
-    def last(o, q):
-        return pltpu.make_async_remote_copy(
-            src_ref=zrecv.at[o], dst_ref=fin.at[c],
-            send_sem=fin_send.at[q], recv_sem=fin_recv.at[q],
-            device_id=(2 * lax.rem(c + q, chips) + k, t),
-            device_id_type=pl.DeviceIdType.MESH,
-        )
-
-    groups = float(2 * chips)
-    for o in range(n):
-        if o > 0:
-            az[o].wait_recv()
-        block = lax.rem(t + o, n)
-
-        @pl.when(block != c)
-        def _():
-            last(o, lax.rem(block + chips - c, chips)).start()
-
-        @pl.when(block == c)
-        def _():
-            gw[rows(c, prows), :] = zrecv[o].astype(f32) / groups
 
     for q in range(1, chips):
         last(0, q).wait_recv()

time: 59.6 us -> 58 us (0.973)
  the two profiles are of different devices: /device:TPU:18 before, /device:TPU:0 now
where the time goes in v3:
time: 58 us; the launch traced here: 57.9 us
  Pallas kernels  57.2 us (99%)
  between operations  0.64 us (1%)
    pallas_call x1, Pallas kernels, fused(): pl.pallas_call(functools.partial(fused_kernel, n, chips), out_shape=(pltp...  56 us
    pallas_call x1, Pallas kernels, fused(): pl.pallas_call(write_out, out_shape=tuple((jax.ShapeDtypeStruct(r.shape,...  1.25 us

profile of v3, /device:TPU:0, one launch (start us, length us, event | category | flops | bytes accessed | tf_op | source)
XLA Modules:
  0.0 57.9 jit_solution(14441454304201027110)
XLA Ops:
  0.6 56.0 %shard_map.84 = (bf16[256,1536]{1,0:T(8,128)(2,1)S(1)}, f32[768,256]{1,0:T(8,128)S(1)}, bf16[256,256]{1,0:T(8,128)(2,1)S(1)}, bf16[256,256]{1,0:T(8,128)(2,1)S(1)}) custom-call(bf16[256,1536]{1,0:T(8,128)(2,1)} %x.1, bf16[256,256]{1,0:T(8,128)(2,1)} %queries.1, bf16[256,256]{1,0:T(8,128)(2,1)} %keys.1, bf16[6144,256]{1,0:T(8,128)(2,1)} %w.1, bf16[256,256]{1,0:T(8,128)(2,1)} %ga.1), custom_call_target="tpu_custom_call" | custom-call | tf_op jit(solution)/shard_map/pallas_call | solution.py:267
  56.6 1.3 %shard_map.85 = (bf16[256,1536]{1,0:T(8,128)(2,1)}, f32[768,256]{1,0:T(8,128)}, bf16[256,256]{1,0:T(8,128)(2,1)}, bf16[256,256]{1,0:T(8,128)(2,1)}) custom-call(bf16[256,1536]{1,0:T(8,128)(2,1)S(1)} %get-tuple-element.8.refs_0_, f32[768,256]{1,0:T(8,128)S(1)} %get-tuple-element.9.refs_1_, bf16[256,256]{1,0:T(8,128)(2,1)S(1)} %get-tuple-element.10.refs_2_, ...), custom_call_target="tpu_custom_call" | custom-call | tf_op jit(solution)/shard_map/pallas_call | solution.py:301
